TPU v7x, 32 devices: a whole 2x2x4 slice. The times are simulated.
32 devices in a mesh: row: 4 (over z), col: 4 (over x, core), depth: 2 (over y).
Axes of the slice: x: 2, y: 2, z: 4, core: 2. Of those that a mesh axis runs over, the one named last changes fastest.
Arguments:
- heads_concat: bfloat16 [2048, 16384], P('row', ('depth', 'col')), may hold values from -6 to 6
- w_out: bfloat16 [16384, 7168], P(('depth', 'row'), 'col'), may hold values from -0.046875 to 0.046875
Outputs:
- projected: bfloat16 [2048, 7168], P('row', ('col', 'depth'))
All inputs are finite; a program needn't handle non-finite values.
Results may differ from a plain program's by a relative error of at most 0.001.
Values may be sent and summed in bfloat16 or wider, within the bound.
A program may use at most 128 MiB of HBM per device.

v0:
```python
import jax
import jax.numpy as jnp
from jax import lax
from jax.sharding import PartitionSpec as P


def per_device(heads_concat, w_out):
    head_half = lax.all_gather(heads_concat, "col", axis=1, tiled=True)
    weight_half = lax.all_gather(w_out, "row", axis=0, tiled=True)
    partial_sum = jnp.dot(head_half, weight_half, preferred_element_type=jnp.float32)
    summed = lax.psum_scatter(partial_sum, "depth", scatter_dimension=1, tiled=True)
    return summed.astype(jnp.bfloat16)


def solution(mesh):
    return jax.shard_map(
        per_device,
        mesh=mesh,
        in_specs=(P("row", ("depth", "col")), P(("depth", "row"), "col")),
        out_specs=P("row", ("col", "depth")),
        check_vma=False,
    )
```

profile of v0, /device:TPU:0, one launch (start us, length us, event | category | flops | bytes accessed | tf_op | source)
XLA Modules:
  0.0 643.9 jit_solution(13111015978111093550)
XLA Ops:
  6.5 0.0 all-gather.3.cloned.1.call-start
  6.5 0.7 all-gather.3.cloned.1.call-update
  7.3 0.0 all-gather.5.cloned.1.call-start
  7.3 0.7 all-gather.5.cloned.1.call-update
  8.0 0.0 reduce-scatter.2.cloned.1.call-start
  8.1 61.9 %all-gather.3.cloned.1.call-done = bf16[512,8192]{1,0:T(8,128)(2,1)} async-done(((bf16[512,2048]{1,0:T(8,128)(2,1)}), bf16[512,8192]{1,0:T(8,128)(2,1)}) %all-gather.3.cloned.1.call-update) | async-done | bytes 8388624 | tf_op jit(solution)/shard_map/all_gather | solution.py:8
  69.9 494.7 %all-gather.5.cloned.1.call-done = bf16[8192,1792]{1,0:T(8,128)(2,1)} async-done(((bf16[2048,1792]{1,0:T(8,128)(2,1)}), bf16[8192,1792]{1,0:T(8,128)(2,1)}) %all-gather.5.cloned.1.call-update) | async-done | bytes 29360144 | tf_op jit(solution)/shard_map/all_gather | solution.py:9
  564.6 22.7 %fusion = f32[512,1792]{1,0:T(8,128)} fusion(bf16[512,8192]{1,0:T(8,128)(2,1)} %all-gather.3.cloned.1.call-done, bf16[8192,1792]{1,0:T(8,128)(2,1)} %all-gather.5.cloned.1.call-done), kind=kOutput, calls=%fused_computation | convolution fusion | flops 15032385536 | bytes 41418752 | tf_op jit(solution)/shard_map/dot_general | solution.py:10
  587.3 0.0 reduce-scatter.2.cloned.1.call-update
  587.3 47.5 %reduce-scatter.2.cloned.1.call-done = f32[512,896]{1,0:T(8,128)} async-done(((f32[512,1792]{1,0:T(8,128)}), f32[512,896]{1,0:T(8,128)}) %reduce-scatter.2.cloned.1.call-update) | async-done | bytes 1835024 | tf_op jit(solution)/shard_map/reduce_scatter | solution.py:11
  634.9 2.5 convert_element_type.3
Async XLA Ops:
  6.5 63.4 %all-gather.3.cloned.1.call-start = ((), (), s32[]{:S(2)}) async-start(), calls=%async_computation.1 | async-start | bytes 10485760 | tf_op jit(solution)/shard_map/all_gather | solution.py:8
  7.3 557.4 %all-gather.5.cloned.1.call-start = ((), (), s32[]{:S(2)}) async-start(), calls=%async_computation.2 | async-start | bytes 36700160 | tf_op jit(solution)/shard_map/all_gather | solution.py:9
  8.0 626.9 %reduce-scatter.2.cloned.1.call-start = ((), (), s32[]{:S(2)}) async-start(), calls=%async_computation.3 | async-start | bytes 5505024 | tf_op jit(solution)/shard_map/reduce_scatter | solution.py:11
Sparse Core Ops, SparseCore 0:
  8.9 60.9 all-gather.2
  71.5 493.0 all-gather.4
  587.4 47.3 reduce-scatter.1
where the time goes:
time: 644 us
  waiting for transfers between devices  606 us (94%)
  matrix products  22.7 us (4%)
  between operations  13.1 us (2%)
    all_gather x1, waiting for transfers between devices, per_device(): weight_half = lax.all_gather(w_out, 'row', axis=0, tiled=True)  495 us
    all_gather x1, waiting for transfers between devices, per_device(): head_half = lax.all_gather(heads_concat, 'col', axis=1, tiled=True)  61.9 us
    reduce_scatter x1, waiting for transfers between devices, per_device(): lax.psum_scatter(partial_sum, 'depth', scatter_dimension=1, tiled=True)  47.5 us
    dot_general x1, matrix products, per_device(): jnp.dot(head_half, weight_half, preferred_element_type=jnp.float32)  22.7 us
  transfers between devices with their start and end apart: 3, of which 3 were waited for; matrix products, arithmetic and copies ran while one was open for 0% of the time, Pallas kernels for 0%

commit v1 on v0

--- a/solution.py
+++ b/solution.py
@@ -4,8 +4,13 @@
 from jax.sharding import PartitionSpec as P
 
 
+def all_parts(x, name, d):
+    blocks = lax.all_gather(x, name)
+    return jnp.concatenate(blocks, axis=d)
+
+
 def per_device(heads_concat, w_out):
-    head_half = lax.all_gather(heads_concat, "col", axis=1, tiled=True)
+    head_half = all_parts(heads_concat, "col", 1)
     weight_half = lax.all_gather(w_out, "row", axis=0, tiled=True)
     partial_sum = jnp.dot(head_half, weight_half, preferred_element_type=jnp.float32)
     summed = lax.psum_scatter(partial_sum, "depth", scatter_dimension=1, tiled=True)

time: 644 us -> 645 us (level)
  waiting for transfers between devices: 606 us -> 594 us
  local copies, waits for them, and re-layouts: 0 us -> 11.7 us
    all_gather x1, waiting for transfers between devices: 495 us -> 483 us  [per_device(): weight_half = lax.all_gather(w_out, 'row', axis=0, tiled=True)]
    reshape x0 -> x1, local copies, waits for them, and re-layouts: none -> 11.7 us  [all_parts(): return jnp.concatenate(blocks, axis=d)]
  transfers between devices with their start and end apart: 3 -> 3, of which waited for: 3 -> 3; matrix products, arithmetic and copies ran while one was open for 0% -> 2% of each run, Pallas kernels for 0% -> 0%
where the time goes in v1:
time: 645 us; the launch traced here: 644 us
  waiting for transfers between devices  594 us (92%)
  matrix products  22.9 us (4%)
  between operations  13.1 us (2%)
  local copies, waits for them, and re-layouts  11.7 us (2%)
    all_gather x1, waiting for transfers between devices, per_device(): weight_half = lax.all_gather(w_out, 'row', axis=0, tiled=True)  483 us
    all_gather x1, waiting for transfers between devices, all_parts(): blocks = lax.all_gather(x, name)  61.9 us
    reduce_scatter x1, waiting for transfers between devices, per_device(): lax.psum_scatter(partial_sum, 'depth', scatter_dimension=1, tiled=True)  47.5 us
    dot_general x1, matrix products, per_device(): jnp.dot(head_half, weight_half, preferred_element_type=jnp.float32)  22.9 us
  transfers between devices with their start and end apart: 3, of which 3 were waited for; matrix products, arithmetic and copies ran while one was open for 2% of the time, Pallas kernels for 0%

profile of v1, /device:TPU:0, one launch (start us, length us, event | category | flops | bytes accessed | tf_op | source)
XLA Modules:
  0.0 644.1 jit_solution(17387813092183159589)
XLA Ops:
  6.5 0.0 all-gather.6.cloned.1.call-start
  6.5 0.7 all-gather.6.cloned.1.call-update
  7.3 0.0 all-gather.4.cloned.1.call-start
  7.3 0.7 all-gather.4.cloned.1.call-update
  8.0 0.0 reduce-scatter.2.cloned.1.call-start
  8.1 61.9 %all-gather.6.cloned.1.call-done = bf16[2048,2048]{1,0:T(8,128)(2,1)} async-done(((bf16[512,2048]{1,0:T(8,128)(2,1)}), bf16[2048,2048]{1,0:T(8,128)(2,1)}) %all-gather.6.cloned.1.call-update) | async-done | bytes 8388624 | tf_op jit(solution)/shard_map/all_gather | solution.py:8
  69.9 11.7 %copy.3 = bf16[512,4,2048]{0,2,1:T(8,128)(2,1)} copy(bf16[512,4,2048]{2,0,1:T(8,128)(2,1)} %bitcast.6) | data formatting | bytes 16777216 | tf_op jit(solution)/shard_map/reshape | solution.py:9
  81.6 483.0 %all-gather.4.cloned.1.call-done = bf16[8192,1792]{1,0:T(8,128)(2,1)} async-done(((bf16[2048,1792]{1,0:T(8,128)(2,1)}), bf16[8192,1792]{1,0:T(8,128)(2,1)}) %all-gather.4.cloned.1.call-update) | async-done | bytes 29360144 | tf_op jit(solution)/shard_map/all_gather | solution.py:14
  564.6 22.9 %fusion = f32[512,1792]{1,0:T(8,128)} fusion(bf16[512,8192]{0,1:T(8,128)(2,1)} %bitcast.7, bf16[8192,1792]{1,0:T(8,128)(2,1)} %all-gather.4.cloned.1.call-done), kind=kOutput, calls=%fused_computation | convolution fusion | flops 15032385536 | bytes 41418752 | tf_op jit(solution)/shard_map/dot_general | solution.py:15
  587.5 0.0 reduce-scatter.2.cloned.1.call-update
  587.5 47.5 %reduce-scatter.2.cloned.1.call-done = f32[512,896]{1,0:T(8,128)} async-done(((f32[512,1792]{1,0:T(8,128)}), f32[512,896]{1,0:T(8,128)}) %reduce-scatter.2.cloned.1.call-update) | async-done | bytes 1835024 | tf_op jit(solution)/shard_map/reduce_scatter | solution.py:16
  635.1 2.5 convert_element_type.3
Async XLA Ops:
  6.5 63.4 %all-gather.6.cloned.1.call-start = ((), (), s32[]{:S(2)}) async-start(), calls=%async_computation.3 | async-start | bytes 10485760 | tf_op jit(solution)/shard_map/all_gather | solution.py:8
  7.3 557.4 %all-gather.4.cloned.1.call-start = ((), (), s32[]{:S(2)}) async-start(), calls=%async_computation.1 | async-start | bytes 36700160 | tf_op jit(solution)/shard_map/all_gather | solution.py:14
  8.0 627.1 %reduce-scatter.2.cloned.1.call-start = ((), (), s32[]{:S(2)}) async-start(), calls=%async_computation.2 | async-start | bytes 5505024 | tf_op jit(solution)/shard_map/reduce_scatter | solution.py:16
Sparse Core Ops, SparseCore 0:
  8.9 60.9 all-gather.5
  71.5 493.0 all-gather.3
  587.7 47.3 reduce-scatter.1
